TPU v7x, 64 devices: a 2x2x8 block of a 4x4x8 slice. The times are simulated.
64 devices in a mesh: data: 4 (over x, y), expert: 16 (over z, core).
Axes of the slice: x: 2, y: 2, z: 8, core: 2. Of those that a mesh axis runs over, the one named last changes fastest.
The devices are a block of a 4x4x8 slice.
Arguments:
- x_in: bfloat16 [8192, 1024], P(('data', 'expert')), parts along dimension 0
- expert_idx: int32 [8192, 8], P(('data', 'expert')), parts along dimension 0
- gate_weight: float32 [8192, 8], P(('data', 'expert')), parts along dimension 0
- grad_y: bfloat16 [8192, 1024], P(('data', 'expert')), parts along dimension 0
- w_in: bfloat16 [64, 1024, 512], P('expert')
- w_out: bfloat16 [64, 512, 1024], P('expert')
Outputs:
- output 1: bfloat16 [8192, 1024], P(('data', 'expert')), parts along dimension 0
- output 2: bfloat16 [8192, 1024], P(('data', 'expert')), parts along dimension 0
- output 3: float32 [8192, 8], P(('data', 'expert')), parts along dimension 0
- output 4: bfloat16 [256, 1024, 512], P(('data', 'expert')), parts along dimension 0
- output 5: bfloat16 [256, 512, 1024], P(('data', 'expert')), parts along dimension 0
There are 4 independent parts. A program takes and returns all parts, laid end to end along the dimension named above; an argument that names none is the same for every part.
All inputs are finite; a program needn't handle non-finite values.
Results may differ from a plain program's by a relative error of at most 0.0100943.
Values are sent between devices in bfloat16 or wider.
A program may use at most 768 MiB of HBM per device.

v0:
```python
import functools

import jax
import jax.numpy as jnp
from jax import lax
from jax.experimental import pallas as pl
from jax.experimental.pallas import tpu as pltpu
from jax.sharding import PartitionSpec as P

CAP_NUM = 5
CAP_DEN = 4
BIG = 3.3e38
F32 = jnp.float32
BF16 = jnp.bfloat16
K0 = 0.7978845608028654
K1 = 0.044715
MESH = pl.DeviceIdType.MESH
VMEM_BYTES = 67_000_000


def split3(v):
    hi = jnp.clip(v, -BIG, BIG).astype(BF16).astype(F32)
    rest = v - hi
    mid = rest.astype(BF16).astype(F32)
    lo = (rest - mid).astype(BF16).astype(F32)
    return hi, mid, lo


def gelu_and_slope(a):
    t = jnp.tanh(K0 * (a + K1 * (a * a * a)))
    cdf = 0.5 * (1.0 + t)
    return a * cdf, cdf + a * (0.5 * (1.0 - t * t)) * (K0 * (1.0 + 3.0 * K1 * (a * a)))


def dot_nn(a, b):
    return lax.dot_general(a, b, (((1,), (0,)), ((), ())), preferred_element_type=F32)


def dot_nt(a, b):
    return lax.dot_general(a, b, (((1,), (1,)), ((), ())), preferred_element_type=F32)


def dot_tn(a, b):
    return lax.dot_general(a, b, (((0,), (0,)), ((), ())), preferred_element_type=F32)


def moe_kernel(chips, cap, n_exp,
               idx_in, gate_in, x_in, dy_in, w1_hbm, w2_hbm,
               y_out, dx_out, dg_out, brow_hbm, hid_hbm, gy_hbm, dact_hbm,
               idx_all, gate_all, xa, dya, vt, cnt, tab, bfeat, grow, brow, gy, hid, slope, orow, dact, pick,
               go, tail, part, spare, sib, ring, mgt, dgp, dgt, dgs, dgr, w1, w2,
               ag_s, ag_r, agb_s, agb_r, in_s, in_r, inb_s, inb_r, rs_s, rs_r, rsb_s, rsb_r,
               dg_s, dg_r, dgb_s, dgb_r, w_sem, o_sem):
    top_k, tok = idx_in.shape
    half = tok // 2
    rows = n_exp * cap
    me = lax.axis_index('expert')
    z = me // 2
    c = me % 2
    far = chips // 2

    def chip(d):
        return (z + d + chips) % chips

    def dev(q, k):
        return {'expert': q * 2 + k}

    right, left, twin = dev(chip(1), c), dev(chip(-1), c), {'expert': z * 2 + 1 - c}
    side = (right, left)
    pending = ([], [])
    outs = []

    def emit(k, src, dst):
        cp = pltpu.make_async_copy(src, dst, o_sem.at[k])
        cp.start()
        outs.append(cp)

    def rcopy(src, dst, ss, rs, to):
        return pltpu.make_async_remote_copy(src_ref=src, dst_ref=dst, send_sem=ss, recv_sem=rs,
                                            device_id=to, device_id_type=MESH)

    def send(src, dst, ss, rs, to):
        cp = rcopy(src, dst, ss, rs, to)
        cp.start()
        return cp

    def landed(dst, ss, rs, to):
        rcopy(dst, dst, ss, rs, to).wait_recv()

    loads = []
    for e in range(n_exp):
        for k, (src, dst) in enumerate(((w1_hbm, w1), (w2_hbm, w2))):
            cp = pltpu.make_async_copy(src.at[e], dst.at[e], w_sem.at[k, e])
            cp.start()
            loads.append(cp)

    barrier = pltpu.get_barrier_semaphore()
    for d in range(1, chips):
        pl.semaphore_signal(barrier, inc=1, device_id=dev(chip(d), c), device_id_type=MESH)
    pl.semaphore_signal(barrier, inc=1, device_id=twin, device_id_type=MESH)
    pl.semaphore_wait(barrier, chips)

    bufs = (xa, dya)
    own = (x_in, dy_in)

    def item(k, h):
        return 2 * (k - 1) + h if k < far else 2 * (far - 1)

    def slot(a, q, h, k=None):
        kk = c if k is None else k
        return bufs[a].at[q, pl.ds(pl.multiple_of(kk * tok + h * half, half), half)]

    def twin_send(a, d, h, src):
        di = d % chips
        pending[a].append(send(src, slot(a, chip(d), h), agb_s.at[a, di, h], agb_r.at[a, di, h], twin))

    def twin_wait(a, d):
        di = d % chips
        for h in range(2):
            landed(slot(a, chip(d), h, 1 - c), agb_s.at[a, di, h], agb_r.at[a, di, h], twin)

    def first_send(a, h):
        src = own[a].at[pl.ds(h * half, half)]
        for r in range(2):
            i = item(1, h)
            pending[a].append(send(src, slot(a, z, h), ag_s.at[a, r, i], ag_r.at[a, r, i], side[r]))

    def poll(a, k, h, r):
        q = chip(-k) if r == 0 else chip(k)
        i = item(k, h)
        here = slot(a, q, h)
        landed(here, ag_s.at[a, r, i], ag_r.at[a, r, i], side[r])
        if k + 1 < far or (k + 1 == far and h == r):
            j = item(k + 1, h)
            pending[a].append(send(here, slot(a, q, h), ag_s.at[a, r, j], ag_r.at[a, r, j], side[r]))
        twin_send(a, (-k if r == 0 else k), h, here)

    def poll2(a, k, h):
        if k == far:
            poll(a, k, h, h)
        else:
            poll(a, k, h, 0)
            poll(a, k, h, 1)

    small = ((idx_in, idx_all), (gate_in, gate_all))
    for d in range(1, chips):
        for s, (src, dst) in enumerate(small):
            pending[1].append(send(src, dst.at[c, z], in_s.at[s, d], in_r.at[s, d], dev(chip(d), c)))
    first_send(0, 0)
    first_send(0, 1)
    first_send(1, 0)
    for src, dst in small:
        dst[c, z] = src[...]
    xa[z, pl.ds(pl.multiple_of(c * tok, tok), tok)] = x_in[...]
    dya[z, pl.ds(pl.multiple_of(c * tok, tok), tok)] = dy_in[...]
    for a in range(2):
        for h in range(2):
            twin_send(a, 0, h, own[a].at[pl.ds(h * half, half)])
    for s, (src, dst) in enumerate(small):
        for d in range(1, chips):
            landed(dst.at[c, chip(-d)], in_s.at[s, d], in_r.at[s, d], twin)
        pending[1].append(send(dst.at[c], dst.at[c], inb_s.at[s], inb_r.at[s], twin))
    poll2(0, 1, 0)
    for s, (src, dst) in enumerate(small):
        landed(dst.at[1 - c], inb_s.at[s], inb_r.at[s], twin)

    first_e = (me * n_exp).astype(F32)
    sub8 = lax.broadcasted_iota(jnp.int32, (8, tok), 0)

    def count_block(b, carry):
        k, q = b // chips, b % chips
        loc = idx_all[k, q].astype(F32) - first_e
        for e in range(n_exp):
            s = jnp.sum(jnp.where(loc == e, 1.0, 0.0), axis=0, keepdims=True)
            cnt[b, e:e + 1, :] = s
            cnt[b, n_exp + e:n_exp + e + 1, :] = s
        return carry

    lax.fori_loop(0, 2 * chips, count_block, 0)
    cmat = cnt[...].reshape(2 * chips * 8, tok)
    ri = lax.broadcasted_iota(jnp.int32, (tok, tok), 0)
    ci = lax.broadcasted_iota(jnp.int32, (tok, tok), 1)
    upper = jnp.where(ri < ci, 1.0, 0.0).astype(BF16)
    rb, cb = ri // 8, ci // 8
    r_ord, c_ord = 2 * (rb % chips) + rb // chips, 2 * (cb % chips) + cb // chips
    prior = jnp.where((c_ord < r_ord) & (ri % 8 == ci % 8), 1.0, 0.0).astype(BF16)
    cbf = cmat.astype(BF16)
    start = dot_nn(cbf, upper) + jnp.sum(dot_nn(prior, cbf), axis=1, keepdims=True)
    cnt[...] = start.reshape(2 * chips, 8, tok)
    row8 = ri % 8
    edge = jnp.where(row8 < n_exp, start, start + cmat)
    edge = jnp.minimum(edge, float(cap)) + (row8 % n_exp).astype(F32) * cap
    vt[...] = edge.reshape(2 * chips, 8, tok)
    poll2(0, 1, 1)

    def table_block(b, carry):
        k, q = b // chips, b % chips
        idx = idx_all[k, q].astype(F32)
        loc = idx - first_e
        at = jnp.zeros((top_k, tok), F32)
        for e in range(n_exp):
            at = at + jnp.where(loc == e, cnt[b, e:e + 1, :], 0.0)
        for j in range(top_k - 1):
            at = at + jnp.where((idx[j:j + 1, :] == idx) & (sub8 > j), 1.0, 0.0)
        ok = (loc >= 0.0) & (loc < n_exp) & (at < cap)
        rr = loc * cap + at
        coarse = jnp.floor(rr * 0.125)
        hi, mid, lo = split3(gate_all[k, q])
        code = jnp.where(ok, coarse - rows // 16, 200.0)
        fine = jnp.where(ok, rr - 8.0 * coarse, 0.0)
        tile = jnp.concatenate([hi, mid, lo, code, fine, jnp.zeros((tok - 40, tok), F32)], axis=0)
        tab[q, :, pl.ds(pl.multiple_of(k * tok, tok), tok)] = tile.astype(BF16)
        return carry

    lax.fori_loop(0, 2 * chips, table_block, 0)

    def esl(e):
        return pl.ds(pl.multiple_of(e * cap, cap), cap)

    def pick_rows(q, e):
        r = (lax.broadcasted_iota(jnp.int32, (cap, tok), 0) + e * cap).astype(F32)
        out = []
        for k in range(2):
            b = k * chips + q
            lo = vt[b, pl.ds(e, 1), :]
            hi = vt[b, pl.ds(e + n_exp, 1), :]
            out.append(jnp.where((r >= lo) & (r < hi), 1.0, 0.0).astype(BF16))
        return jnp.concatenate(out, axis=1)

    def gather_step(a, d):
        twin_wait(a, d)
        q = chip(d)
        dst = brow if a == 0 else gy

        def body(e, carry):
            if a == 0:
                pick[q, esl(e), :] = pick_rows(q, e)
            p = pick[q, esl(e), :]
            g = dot_nn(p, bufs[a][q]).astype(BF16)
            if d == 0:
                dst[esl(e), :] = g
            else:
                dst[esl(e), :] = dst[esl(e), :] + g
            if a == 0:
                f = dot_nt(p, tab[q])
                bfeat[esl(e), :] = f if d == 0 else bfeat[esl(e), :] + f
            return carry

        lax.fori_loop(0, n_exp, body, 0)

    gather_step(0, 0)
    poll2(0, 2, 0)
    gather_step(0, -1)
    poll2(0, 2, 1)
    gather_step(0, 1)
    poll2(0, 3, 0)
    gather_step(0, -2)
    poll2(0, 3, 1)
    first_send(1, 1)
    poll2(1, 1, 0)
    gather_step(0, 2)
    poll2(0, 4, 0)
    poll2(0, 4, 1)
    gather_step(0, -3)
    gather_step(0, 3)
    poll2(1, 1, 1)
    gather_step(0, 4)

    for cp in loads:
        cp.wait()

    def forward(e):
        act, sl = gelu_and_slope(dot_nn(brow[esl(e), :], w1[e]))
        hb = act.astype(BF16)
        hid[esl(e), :] = hb
        slope[esl(e), :] = sl
        orow[esl(e), :] = dot_nn(hb, w2[e]).astype(BF16)

    def forward_pair(e0):
        def body(i, carry):
            forward(e0 + i)
            return carry
        lax.fori_loop(0, 2, body, 0)

    forward_pair(0)
    poll2(1, 2, 0)
    forward_pair(2)
    emit(0, brow, brow_hbm)
    emit(1, hid, hid_hbm)

    lane = lax.broadcasted_iota(jnp.int32, (tok, tok), 1)

    def gate_rows(i, carry):
        sl = pl.ds(pl.multiple_of(i * tok, tok), tok)
        f = bfeat[sl, :]
        r = ri + i * tok
        want_c = (r // 8 - rows // 16).astype(F32)
        want_f = (r % 8).astype(F32)
        hit = (pltpu.roll(f, tok - 24, 1) == want_c) & (pltpu.roll(f, tok - 32, 1) == want_f) & (lane < top_k)
        val = f + pltpu.roll(f, tok - 8, 1) + pltpu.roll(f, tok - 16, 1)
        g = jnp.sum(jnp.where(hit, val, 0.0), axis=1, keepdims=True)
        bfeat[sl, :] = jnp.where(lane == top_k, g, jnp.where(hit, 1.0, 0.0))
        hi, mid, lo = split3(g)
        cols = jnp.where(lane == 0, hi, jnp.where(lane == 1, mid, jnp.where(lane == 2, lo, 0.0)))
        grow[i] = jnp.transpose(cols)[0:8, :]
        return carry

    lax.fori_loop(0, rows // tok, gate_rows, 0)
    poll2(1, 2, 1)

    order = [far]
    for d in range(far - 1, 0, -1):
        order += [d, -d]
    order.append(0)
    place = {d: i for i, d in enumerate(order)}
    place[-far] = 0
    own_wait, twin_wait_s = {}, {}
    n_cols = x_in.shape[1]
    tile = xa.shape[1]
    wide = xa.shape[2]
    blocks = rows // tok
    main = wide // tok

    def mtile(m):
        return pl.ds(pl.multiple_of(m * tile, tile), tile)

    def scale_rows(j, carry):
        js = pl.ds(pl.multiple_of(j * tok, tok), tok)
        m = j // (tile // tok)
        ms = pl.ds(pl.multiple_of((j % (tile // tok)) * tok, tok), tok)
        for i in range(blocks):
            t = jnp.transpose(orow[i * tok:(i + 1) * tok, js]).astype(F32)
            hi, mid, lo = split3(t * jnp.sum(grow[i, 0:3, :], axis=0, keepdims=True))
            go[js, i * tok:(i + 1) * tok] = hi.astype(BF16)
            for s, v in enumerate((mid, lo)):
                if i < main:
                    xa[s * (n_cols // tile) + m, ms, i * tok:(i + 1) * tok] = v.astype(BF16)
                else:
                    tail[s, js, (i - main) * tok:(i - main + 1) * tok] = v.astype(BF16)
        return carry

    def flip_rows(j, carry):
        js = pl.ds(pl.multiple_of(j * tok, tok), tok)
        for i in range(blocks):
            go[js, i * tok:(i + 1) * tok] = jnp.transpose(orow[i * tok:(i + 1) * tok, js])
        return carry

    def chunk(a, d):
        q, di = chip(d), place[d]
        sp = di % spare.shape[0]
        for cp in own_wait.pop(di, []):
            cp.wait_send()
        if sp in twin_wait_s:
            twin_wait_s.pop(sp).wait_send()

        def body(m, carry):
            ms = mtile(m)
            r = dot_nn(go[ms, :], pick[q])
            if a == 0:
                for s in range(2):
                    r = r + dot_nn(xa[s * (n_cols // tile) + m], pick[q, 0:wide, :])
                    r = r + dot_nn(tail[s, ms, :], pick[q, wide:rows, :])
            r0, r1 = r[:, 0:tok], r[:, tok:2 * tok]
            part[di, ms, :] = jnp.where(c == 0, r0, r1)
            spare[sp, ms, :] = jnp.where(c == 0, r1, r0)
            return carry

        lax.fori_loop(0, n_cols // tile, body, 0)
        twin_wait_s[sp] = send(spare.at[sp], sib.at[a, di], rsb_s.at[a, di], rsb_r.at[a, di], twin)
        if a == 1:
            t = dot_nn(mgt[...], pick[q])
            t = t[0:8] + t[8:16] + t[16:24]
            dgp[q] = jnp.where(c == 0, t[:, 0:tok], t[:, tok:2 * tok])
            dgt[q] = jnp.where(c == 0, t[:, tok:2 * tok], t[:, 0:tok])

    hd = n_cols // 2

    def mine(d, h):
        return part.at[place[d], pl.ds(h * hd, hd)]

    seen = set()

    def twin_part_wait(a, d):
        di = place[d]
        if (a, di) not in seen:
            seen.add((a, di))
            landed(sib.at[a, di], rsb_s.at[a, di], rsb_r.at[a, di], twin)

    def items(r):
        near, other = (0, 1) if r == 0 else (1, 0)
        out = [(far, near)]
        for d in range(far - 1, 0, -1):
            out += [(d, other), (d, near)]
        return out

    def ring_send(a, i, r):
        d, h = items(r)[i]
        sd = d if r == 0 else -d
        di = place[sd]
        twin_part_wait(a, sd)
        ref = mine(sd, h)
        total = ref[...] + sib[a, di, h * hd:(h + 1) * hd, :]
        if (d + 1, h) in items(r):
            p = items(r).index((d + 1, h))
            landed(ring.at[a, r, p], rs_s.at[a, r, p], rs_r.at[a, r, p], side[r])
            total = total + ring[a, r, p]
        ref[...] = total
        own_wait.setdefault(di, []).append(send(ref, ring.at[a, r, i], rs_s.at[a, r, i], rs_r.at[a, r, i], side[r]))

    def ring_send2(a, i):
        ring_send(a, i, 0)
        ring_send(a, i, 1)

    def finish(a, src, dst):
        twin_part_wait(a, 0)
        for h in range(2):
            total = mine(0, h)[...] + sib[a, place[0], h * hd:(h + 1) * hd, :]
            for r in range(2):
                p = items(r).index((1, h))
                landed(ring.at[a, r, p], rs_s.at[a, r, p], rs_r.at[a, r, p], side[r])
                total = total + ring[a, r, p]
            for j in range(hd // tok):
                cs = slice(h * hd + j * tok, h * hd + (j + 1) * tok)
                dst[:, cs] = (src[:, cs].astype(F32) + jnp.transpose(total[j * tok:(j + 1) * tok, :])).astype(BF16)

    def backward_pair(e0):
        def body(i, carry):
            e = e0 + i
            es = esl(e)
            dyr = gy[es, :].astype(F32)
            f = bfeat[es, :]
            dg = jnp.sum(dyr * orow[es, :].astype(F32), axis=1, keepdims=True)
            lane_e = lax.broadcasted_iota(jnp.int32, (cap, tok), 1)
            hi, mid, lo = split3(jnp.where(lane_e < top_k, f * dg, 0.0))
            bfeat[es, :] = hi + pltpu.roll(mid, 8, 1) + pltpu.roll(lo, 16, 1)
            g = (f[:, top_k:top_k + 1] * dyr).astype(BF16)
            gy[es, :] = g
            dh = dot_nt(g, w2[e]).astype(BF16)
            da = (dh.astype(F32) * slope[es, :]).astype(BF16)
            dact[es, :] = da
            orow[es, :] = dot_nt(da, w1[e]).astype(BF16)
            return carry
        lax.fori_loop(0, 2, body, 0)

    def gate_cols(i, carry):
        sl = pl.ds(pl.multiple_of(i * tok, tok), tok)
        mgt[:, sl] = jnp.transpose(bfeat[sl, :])[0:mgt.shape[0], :].astype(BF16)
        return carry

    for cp in pending[0]:
        cp.wait_send()
    lax.fori_loop(0, n_cols // tok, scale_rows, 0)
    poll2(1, 3, 0)
    chunk(0, far)
    poll2(1, 3, 1)
    chunk(0, 3)
    ring_send2(0, 0)
    chunk(0, -3)
    ring_send2(0, 1)
    poll2(1, 4, 0)
    poll2(1, 4, 1)
    chunk(0, 2)
    chunk(0, -2)
    ring_send2(0, 2)
    chunk(0, 1)
    chunk(0, -1)
    ring_send2(0, 3)
    chunk(0, 0)
    gather_step(1, 0)
    gather_step(1, -1)
    ring_send2(0, 4)
    for d in (1, -2, 2, -3, 3, 4):
        gather_step(1, d)
    ring_send2(0, 5)
    backward_pair(0)
    ring_send2(0, 6)
    backward_pair(2)
    emit(2, gy, gy_hbm)
    emit(3, dact, dact_hbm)
    lax.fori_loop(0, blocks, gate_cols, 0)
    lax.fori_loop(0, n_cols // tok, flip_rows, 0)
    chunk(1, far)
    chunk(1, 3)
    ring_send2(1, 0)
    chunk(1, -3)
    ring_send2(1, 1)
    chunk(1, 2)
    chunk(1, -2)
    chunk(1, 1)
    chunk(1, -1)
    finish(0, x_in, y_out)
    ring_send2(1, 2)
    chunk(1, 0)
    dg_cp = send(dgt, dgs, dgb_s.at[0], dgb_r.at[0], twin)
    ring_send2(1, 3)
    landed(dgs, dgb_s.at[0], dgb_r.at[0], twin)
    dgp[...] = dgp[...] + dgs[...]
    dg_sends = [send(dgp.at[chip(d)], dgr.at[z], dg_s.at[d], dg_r.at[d], dev(chip(d), c)) for d in range(1, chips)]
    ring_send2(1, 4)
    ring_send2(1, 5)
    ring_send2(1, 6)
    dg_total = dgp[z]
    for d in range(1, chips):
        landed(dgr.at[chip(-d)], dg_s.at[d], dg_r.at[d], twin)
        dg_total = dg_total + dgr[chip(-d)]
    dg_out[...] = dg_total
    finish(1, dy_in, dx_out)
    dg_cp.wait_send()
    for group in (dg_sends, pending[1], list(twin_wait_s.values()), *own_wait.values()):
        for cp in group:
            cp.wait_send()
    for cp in outs:
        cp.wait()


def weight_kernel(y_ref, dx_ref, dg_ref, brow, hid, gy, dact, y_out, dx_out, dg_out, dw1, dw2):
    @pl.when(pl.program_id(0) == 0)
    def _():
        y_out[...] = y_ref[...]
        dx_out[...] = dx_ref[...]
        dg_out[...] = dg_ref[...]

    dw2[0] = dot_tn(hid[...], gy[...]).astype(BF16)
    dw1[0] = dot_tn(brow[...], dact[...]).astype(BF16)


def solution(mesh):
    groups = mesh.shape['expert']
    tok_spec = P(('data', 'expert'), None)
    weight_spec = P('expert', None, None)
    grad_spec = P(('data', 'expert'), None, None)

    def device_pass(x_in, expert_idx, gate_weight, grad_y, w_in, w_out):
        tok, top_k = expert_idx.shape
        n_exp, dm, ff = w_in.shape
        n_pairs = tok * top_k
        cap = (CAP_NUM * n_pairs) // (CAP_DEN * n_exp)
        rows = n_exp * cap
        chips = groups // 2
        vmem = pl.BlockSpec(memory_space=pltpu.VMEM)
        hbm = pl.BlockSpec(memory_space=pl.ANY)
        dma = pltpu.SemaphoreType.DMA
        shape = jax.ShapeDtypeStruct
        small = (shape((tok, dm), BF16), shape((tok, dm), BF16), shape((top_k, tok), F32))
        mids = pl.pallas_call(
            functools.partial(moe_kernel, chips, cap, n_exp),
            name='moe',
            out_shape=small + (shape((rows, dm), BF16), shape((rows, ff), BF16), shape((rows, dm), BF16), shape((rows, ff), BF16)),
            in_specs=[vmem, vmem, vmem, vmem, hbm, hbm],
            out_specs=(vmem, vmem, vmem, hbm, hbm, hbm, hbm),
            scratch_shapes=[
                pltpu.VMEM((2, chips, top_k, tok), jnp.int32),
                pltpu.VMEM((2, chips, top_k, tok), F32),
                pltpu.VMEM((chips, 2 * tok, dm), BF16),
                pltpu.VMEM((chips, 2 * tok, dm), BF16),
                pltpu.VMEM((2 * chips, 8, tok), F32),
                pltpu.VMEM((2 * chips, 8, tok), F32),
                pltpu.VMEM((chips, tok, 2 * tok), BF16),
                pltpu.VMEM((rows, tok), F32),
                pltpu.VMEM((rows // tok, 8, tok), F32),
                pltpu.VMEM((rows, dm), BF16),
                pltpu.VMEM((rows, dm), BF16),
                pltpu.VMEM((rows, ff), BF16),
                pltpu.VMEM((rows, ff), F32),
                pltpu.VMEM((rows, dm), BF16),
                pltpu.VMEM((rows, ff), BF16),
                pltpu.VMEM((chips, rows, 2 * tok), BF16),
                pltpu.VMEM((dm, rows), BF16),
                pltpu.VMEM((2, dm, rows - dm), BF16),
                pltpu.VMEM((chips, dm, tok), F32),
                pltpu.VMEM((4, dm, tok), F32),
                pltpu.VMEM((2, chips, dm, tok), F32),
                pltpu.VMEM((2, 2, chips - 1, dm // 2, tok), F32),
                pltpu.VMEM((32, rows), BF16),
                pltpu.VMEM((chips, 8, tok), F32),
                pltpu.VMEM((chips, 8, tok), F32),
                pltpu.VMEM((chips, 8, tok), F32),
                pltpu.VMEM((chips, 8, tok), F32),
                pltpu.VMEM((n_exp, dm, ff), BF16),
                pltpu.VMEM((n_exp, ff, dm), BF16),
                dma((2, 2, chips - 1)), dma((2, 2, chips - 1)),
                dma((2, chips, 2)), dma((2, chips, 2)),
                dma((2, chips)), dma((2, chips)), dma((2,)), dma((2,)),
                dma((2, 2, chips - 1)), dma((2, 2, chips - 1)),
                dma((2, chips)), dma((2, chips)),
                dma((chips,)), dma((chips,)), dma((1,)), dma((1,)),
                dma((2, n_exp)), dma((4,)),
            ],
            compiler_params=pltpu.CompilerParams(collective_id=0, has_side_effects=True,
                                                 vmem_limit_bytes=VMEM_BYTES),
        )(expert_idx.T, gate_weight.T, x_in, grad_y, w_in, w_out)
        y, dx, dg, dw1, dw2 = pl.pallas_call(
            weight_kernel,
            name='weights',
            grid=(n_exp,),
            out_shape=small + (shape((n_exp, dm, ff), BF16), shape((n_exp, ff, dm), BF16)),
            in_specs=[pl.BlockSpec((tok, dm), lambda e: (0, 0)), pl.BlockSpec((tok, dm), lambda e: (0, 0)),
                      pl.BlockSpec((top_k, tok), lambda e: (0, 0)),
                      pl.BlockSpec((cap, dm), lambda e: (e, 0)), pl.BlockSpec((cap, ff), lambda e: (e, 0)),
                      pl.BlockSpec((cap, dm), lambda e: (e, 0)), pl.BlockSpec((cap, ff), lambda e: (e, 0))],
            out_specs=(pl.BlockSpec((tok, dm), lambda e: (0, 0)), pl.BlockSpec((tok, dm), lambda e: (0, 0)),
                       pl.BlockSpec((top_k, tok), lambda e: (0, 0)),
                       pl.BlockSpec((1, dm, ff), lambda e: (e, 0, 0)), pl.BlockSpec((1, ff, dm), lambda e: (e, 0, 0))),
        )(*mids)
        return y, dx, dg.T, dw1, dw2

    return jax.shard_map(device_pass, mesh=mesh,
                         in_specs=(tok_spec, tok_spec, tok_spec, tok_spec, weight_spec, weight_spec),
                         out_specs=(tok_spec, tok_spec, tok_spec, grad_spec, grad_spec), check_vma=False)
```

profile of v0, /device:TPU:21, one launch (start us, length us, event | category | flops | bytes accessed | tf_op | source)
XLA Modules:
  0.0 156.8 jit_solution(5057166760680410767)
XLA Ops:
  0.6 147.2 %moe.1 = (bf16[128,1024]{1,0:T(8,128)(2,1)}, bf16[128,1024]{1,0:T(8,128)(2,1)}, f32[8,128]{1,0:T(8,128)}, bf16[1280,1024]{1,0:T(8,128)(2,1)}, bf16[1280,512]{1,0...) custom-call(s32[8,128]{1,0:T(8,128)} %bitcast.3, f32[8,128]{1,0:T(8,128)} %bitcast.4, ...), custom_call_target="tpu_custom_call" | custom-call | tf_op jit(solution)/shard_map/moe/pallas_call | solution.py:545
  147.9 9.0 %weights.1 = (bf16[128,1024]{1,0:T(8,128)(2,1)}, bf16[128,1024]{1,0:T(8,128)(2,1)}, f32[8,128]{1,0:T(8,128)}, bf16[4,1024,512]{2,1,0:T(8,128)(2,1)}, bf16[4,512,1024]{2,1,0:T(8,128)(2,1)}) custom-call(bf16[128,1024]{1,0:T(8,128)(2,1)} %get-tuple-element.17.y_ref, bf16[128,1024]{1,0:T(8,128)(2,1)} %get-tuple-element.18.dx_ref, ...), custom_call_target="tpu_custom_call" | custom-call | tf_op jit(solution)/shard_map/weights/pallas_call | solution.py:592
where the time goes:
time: 157 us
  Pallas kernels  156 us (99%)
    pallas_call x1, Pallas kernels, device_pass(): pl.pallas_call(functools.partial(moe_kernel, chips, cap, n_exp), name='mo...  147 us
    pallas_call x1, Pallas kernels, device_pass(): pl.pallas_call(weight_kernel, name='weights', grid=(n_exp,), out_shape=sm...  8.96 us

commit v1 on v0

--- a/solution.py
+++ b/solution.py
@@ -45,13 +45,13 @@
 
 
 def moe_kernel(chips, cap, n_exp,
-               idx_in, gate_in, x_in, dy_in, w1_hbm, w2_hbm,
-               y_out, dx_out, dg_out, brow_hbm, hid_hbm, gy_hbm, dact_hbm,
-               idx_all, gate_all, xa, dya, vt, cnt, tab, bfeat, grow, brow, gy, hid, slope, orow, dact, pick,
-               go, tail, part, spare, sib, ring, mgt, dgp, dgt, dgs, dgr, w1, w2,
+               idx_hbm, gate_hbm, x_hbm, dy_hbm, w1_hbm, w2_hbm,
+               y_hbm, dx_hbm, dg_hbm, dw1_hbm, dw2_hbm,
+               xs, ys, idx_all, gate_all, xa, dya, vt, cnt, tab, ft, hitm, grow, gcol, brow, gy, hid, slope, orow, dact,
+               pick, go, tail, part, spare, sib, ring, mgt, dgp, dgt, dgs, dgr, w1, w2,
                ag_s, ag_r, agb_s, agb_r, in_s, in_r, inb_s, inb_r, rs_s, rs_r, rsb_s, rsb_r,
-               dg_s, dg_r, dgb_s, dgb_r, w_sem, o_sem):
-    top_k, tok = idx_in.shape
+               dg_s, dg_r, dgb_s, dgb_r, l_sem, w_sem, o_sem, dw_sem):
+    top_k, tok = idx_all.shape[2:]
     half = tok // 2
     rows = n_exp * cap
     me = lax.axis_index('expert')
@@ -87,21 +87,31 @@
     def landed(dst, ss, rs, to):
         rcopy(dst, dst, ss, rs, to).wait_recv()
 
+    own_rows = pl.ds(pl.multiple_of(c * tok, tok), tok)
+    inputs = []
+    for k, (src, dst) in enumerate(((idx_hbm, idx_all.at[c, z]), (gate_hbm, gate_all.at[c, z]), (x_hbm, xs), (dy_hbm, ys),
+                                    (x_hbm, xa.at[z, own_rows]), (dy_hbm, dya.at[z, own_rows]))):
+        cp = pltpu.make_async_copy(src, dst, l_sem.at[k])
+        cp.start()
+        inputs.append(cp)
+
+    barrier = pltpu.get_barrier_semaphore()
+    for d in range(1, chips):
+        pl.semaphore_signal(barrier, inc=1, device_id=dev(chip(d), c), device_id_type=MESH)
+    pl.semaphore_signal(barrier, inc=1, device_id=twin, device_id_type=MESH)
+
     loads = []
     for e in range(n_exp):
         for k, (src, dst) in enumerate(((w1_hbm, w1), (w2_hbm, w2))):
             cp = pltpu.make_async_copy(src.at[e], dst.at[e], w_sem.at[k, e])
             cp.start()
             loads.append(cp)
-
-    barrier = pltpu.get_barrier_semaphore()
-    for d in range(1, chips):
-        pl.semaphore_signal(barrier, inc=1, device_id=dev(chip(d), c), device_id_type=MESH)
-    pl.semaphore_signal(barrier, inc=1, device_id=twin, device_id_type=MESH)
+    for cp in inputs:
+        cp.wait()
     pl.semaphore_wait(barrier, chips)
 
     bufs = (xa, dya)
-    own = (x_in, dy_in)
+    own = (xs, ys)
 
     def item(k, h):
         return 2 * (k - 1) + h if k < far else 2 * (far - 1)
@@ -142,26 +152,22 @@
             poll(a, k, h, 0)
             poll(a, k, h, 1)
 
-    small = ((idx_in, idx_all), (gate_in, gate_all))
+    small = (idx_all, gate_all)
     for d in range(1, chips):
-        for s, (src, dst) in enumerate(small):
-            pending[1].append(send(src, dst.at[c, z], in_s.at[s, d], in_r.at[s, d], dev(chip(d), c)))
+        for s, dst in enumerate(small):
+            pending[1].append(send(dst.at[c, z], dst.at[c, z], in_s.at[s, d], in_r.at[s, d], dev(chip(d), c)))
     first_send(0, 0)
     first_send(0, 1)
     first_send(1, 0)
-    for src, dst in small:
-        dst[c, z] = src[...]
-    xa[z, pl.ds(pl.multiple_of(c * tok, tok), tok)] = x_in[...]
-    dya[z, pl.ds(pl.multiple_of(c * tok, tok), tok)] = dy_in[...]
     for a in range(2):
         for h in range(2):
             twin_send(a, 0, h, own[a].at[pl.ds(h * half, half)])
-    for s, (src, dst) in enumerate(small):
+    for s, dst in enumerate(small):
         for d in range(1, chips):
             landed(dst.at[c, chip(-d)], in_s.at[s, d], in_r.at[s, d], twin)
         pending[1].append(send(dst.at[c], dst.at[c], inb_s.at[s], inb_r.at[s], twin))
     poll2(0, 1, 0)
-    for s, (src, dst) in enumerate(small):
+    for s, dst in enumerate(small):
         landed(dst.at[1 - c], inb_s.at[s], inb_r.at[s], twin)
 
     first_e = (me * n_exp).astype(F32)
@@ -208,7 +214,7 @@
         hi, mid, lo = split3(gate_all[k, q])
         code = jnp.where(ok, coarse - rows // 16, 200.0)
         fine = jnp.where(ok, rr - 8.0 * coarse, 0.0)
-        tile = jnp.concatenate([hi, mid, lo, code, fine, jnp.zeros((tok - 40, tok), F32)], axis=0)
+        tile = jnp.concatenate([hi, mid, lo, code, fine, jnp.zeros((8, tok), F32)], axis=0)
         tab[q, :, pl.ds(pl.multiple_of(k * tok, tok), tok)] = tile.astype(BF16)
         return carry
 
@@ -217,95 +223,82 @@
     def esl(e):
         return pl.ds(pl.multiple_of(e * cap, cap), cap)
 
-    def pick_rows(q, e):
-        r = (lax.broadcasted_iota(jnp.int32, (cap, tok), 0) + e * cap).astype(F32)
-        out = []
-        for k in range(2):
-            b = k * chips + q
-            lo = vt[b, pl.ds(e, 1), :]
-            hi = vt[b, pl.ds(e + n_exp, 1), :]
-            out.append(jnp.where((r >= lo) & (r < hi), 1.0, 0.0).astype(BF16))
-        return jnp.concatenate(out, axis=1)
-
-    def gather_step(a, d):
-        twin_wait(a, d)
-        q = chip(d)
+    ft[...] = jnp.zeros_like(ft)
+
+    def pick_block(q, carry):
+        for e in range(n_exp):
+            r = (lax.broadcasted_iota(jnp.int32, (cap, tok), 0) + e * cap).astype(F32)
+            out = []
+            for k in range(2):
+                b = k * chips + q
+                out.append(jnp.where((r >= vt[b, e:e + 1, :]) & (r < vt[b, n_exp + e:n_exp + e + 1, :]), 1.0, 0.0).astype(BF16))
+            pick[q, e * cap:(e + 1) * cap, :] = jnp.concatenate(out, axis=1)
+        ft[...] = ft[...] + dot_nt(tab[q], pick[q])
+        return carry
+
+    lax.fori_loop(0, chips // 2, pick_block, 0)
+    poll2(0, 2, 0)
+    lax.fori_loop(chips // 2, chips, pick_block, 0)
+    poll2(0, 2, 1)
+    first_send(1, 1)
+
+    r8 = lax.broadcasted_iota(jnp.int32, (top_k, rows), 1)
+    hit = (ft[24:32, :] == ((r8 >> 3) - rows // 16).astype(F32)) & (ft[32:40, :] == (r8 & 7).astype(F32))
+    val = ft[0:8, :] + ft[8:16, :] + ft[16:24, :]
+    hitm[...] = jnp.where(hit, 1.0, 0.0)
+    grow[...] = jnp.broadcast_to(jnp.sum(jnp.where(hit, val, 0.0), axis=0, keepdims=True), (8, rows))
+
+    def gate_col(i, carry):
+        sl = pl.ds(pl.multiple_of(i * tok, tok), tok)
+        gcol[sl, :] = jnp.transpose(jnp.broadcast_to(grow[0:1, sl], (tok, tok)))
+        return carry
+
+    lax.fori_loop(0, rows // tok, gate_col, 0)
+
+    def gather(a, ds, first=False):
+        for d in ds:
+            twin_wait(a, d)
         dst = brow if a == 0 else gy
 
         def body(e, carry):
-            if a == 0:
-                pick[q, esl(e), :] = pick_rows(q, e)
-            p = pick[q, esl(e), :]
-            g = dot_nn(p, bufs[a][q]).astype(BF16)
-            if d == 0:
-                dst[esl(e), :] = g
-            else:
-                dst[esl(e), :] = dst[esl(e), :] + g
-            if a == 0:
-                f = dot_nt(p, tab[q])
-                bfeat[esl(e), :] = f if d == 0 else bfeat[esl(e), :] + f
+            r = None
+            for d in ds:
+                q = chip(d)
+                t = dot_nn(pick[q, esl(e), :], bufs[a][q])
+                r = t if r is None else r + t
+            r = r.astype(BF16)
+            dst[esl(e), :] = r if first else dst[esl(e), :] + r
             return carry
 
         lax.fori_loop(0, n_exp, body, 0)
 
-    gather_step(0, 0)
-    poll2(0, 2, 0)
-    gather_step(0, -1)
-    poll2(0, 2, 1)
-    gather_step(0, 1)
+    gather(0, (0, 1, -1), True)
     poll2(0, 3, 0)
-    gather_step(0, -2)
+    gather(0, (2, -2))
     poll2(0, 3, 1)
-    first_send(1, 1)
     poll2(1, 1, 0)
-    gather_step(0, 2)
     poll2(0, 4, 0)
     poll2(0, 4, 1)
-    gather_step(0, -3)
-    gather_step(0, 3)
     poll2(1, 1, 1)
-    gather_step(0, 4)
+    gather(0, (3, -3, 4))
 
     for cp in loads:
         cp.wait()
 
-    def forward(e):
-        act, sl = gelu_and_slope(dot_nn(brow[esl(e), :], w1[e]))
-        hb = act.astype(BF16)
-        hid[esl(e), :] = hb
-        slope[esl(e), :] = sl
-        orow[esl(e), :] = dot_nn(hb, w2[e]).astype(BF16)
-
     def forward_pair(e0):
         def body(i, carry):
-            forward(e0 + i)
+            e = e0 + i
+            act, sl = gelu_and_slope(dot_nn(brow[esl(e), :], w1[e]))
+            hb = act.astype(BF16)
+            hid[esl(e), :] = hb
+            slope[esl(e), :] = sl
+            orow[esl(e), :] = dot_nn(hb, w2[e]).astype(BF16)
             return carry
         lax.fori_loop(0, 2, body, 0)
 
     forward_pair(0)
     poll2(1, 2, 0)
     forward_pair(2)
-    emit(0, brow, brow_hbm)
-    emit(1, hid, hid_hbm)
-
-    lane = lax.broadcasted_iota(jnp.int32, (tok, tok), 1)
-
-    def gate_rows(i, carry):
-        sl = pl.ds(pl.multiple_of(i * tok, tok), tok)
-        f = bfeat[sl, :]
-        r = ri + i * tok
-        want_c = (r // 8 - rows // 16).astype(F32)
-        want_f = (r % 8).astype(F32)
-        hit = (pltpu.roll(f, tok - 24, 1) == want_c) & (pltpu.roll(f, tok - 32, 1) == want_f) & (lane < top_k)
-        val = f + pltpu.roll(f, tok - 8, 1) + pltpu.roll(f, tok - 16, 1)
-        g = jnp.sum(jnp.where(hit, val, 0.0), axis=1, keepdims=True)
-        bfeat[sl, :] = jnp.where(lane == top_k, g, jnp.where(hit, 1.0, 0.0))
-        hi, mid, lo = split3(g)
-        cols = jnp.where(lane == 0, hi, jnp.where(lane == 1, mid, jnp.where(lane == 2, lo, 0.0)))
-        grow[i] = jnp.transpose(cols)[0:8, :]
-        return carry
-
-    lax.fori_loop(0, rows // tok, gate_rows, 0)
     poll2(1, 2, 1)
 
     order = [far]
@@ -315,7 +308,7 @@
     place = {d: i for i, d in enumerate(order)}
     place[-far] = 0
     own_wait, twin_wait_s = {}, {}
-    n_cols = x_in.shape[1]
+    n_cols = xs.shape[1]
     tile = xa.shape[1]
     wide = xa.shape[2]
     blocks = rows // tok
@@ -330,7 +323,7 @@
         ms = pl.ds(pl.multiple_of((j % (tile // tok)) * tok, tok), tok)
         for i in range(blocks):
             t = jnp.transpose(orow[i * tok:(i + 1) * tok, js]).astype(F32)
-            hi, mid, lo = split3(t * jnp.sum(grow[i, 0:3, :], axis=0, keepdims=True))
+            hi, mid, lo = split3(t * grow[0:1, i * tok:(i + 1) * tok])
             go[js, i * tok:(i + 1) * tok] = hi.astype(BF16)
             for s, v in enumerate((mid, lo)):
                 if i < main:
@@ -428,12 +421,10 @@
             e = e0 + i
             es = esl(e)
             dyr = gy[es, :].astype(F32)
-            f = bfeat[es, :]
+            gc = gcol[es, :]
             dg = jnp.sum(dyr * orow[es, :].astype(F32), axis=1, keepdims=True)
-            lane_e = lax.broadcasted_iota(jnp.int32, (cap, tok), 1)
-            hi, mid, lo = split3(jnp.where(lane_e < top_k, f * dg, 0.0))
-            bfeat[es, :] = hi + pltpu.roll(mid, 8, 1) + pltpu.roll(lo, 16, 1)
-            g = (f[:, top_k:top_k + 1] * dyr).astype(BF16)
+            gcol[es, :] = jnp.broadcast_to(dg, (cap, tok))
+            g = (jnp.concatenate([gc] * (n_cols // tok), axis=1) * dyr).astype(BF16)
             gy[es, :] = g
             dh = dot_nt(g, w2[e]).astype(BF16)
             da = (dh.astype(F32) * slope[es, :]).astype(BF16)
@@ -444,84 +435,132 @@
 
     def gate_cols(i, carry):
         sl = pl.ds(pl.multiple_of(i * tok, tok), tok)
-        mgt[:, sl] = jnp.transpose(bfeat[sl, :])[0:mgt.shape[0], :].astype(BF16)
+        d = jnp.transpose(gcol[sl, :])[0:8, :]
+        hi, mid, lo = split3(jnp.where(hitm[:, sl] > 0.0, d, 0.0))
+        mgt[:, sl] = jnp.concatenate([hi, mid, lo, jnp.zeros_like(hi)], axis=0).astype(BF16)
         return carry
+
+    ff = w1.shape[2]
+    g1, g2 = n_cols // tile, ff // tile
+
+    def weight_copies(e):
+        lo = pl.multiple_of(ff * (e % 2), ff)
+        out = []
+        for s in range(g2):
+            out.append(pltpu.make_async_copy(dya.at[g2 * e + s], dw2_hbm.at[e, pl.ds(s * tile, tile)], dw_sem.at[0, e, s]))
+        for s in range(g1):
+            out.append(pltpu.make_async_copy(xa.at[g1 * (e // 2) + s, :, pl.ds(lo, ff)],
+                                             dw1_hbm.at[e, pl.ds(s * tile, tile)], dw_sem.at[1, e, s]))
+        return out
+
+    def weight_pair(e0):
+        def body(i, carry):
+            e = e0 + i
+            es = esl(e)
+            lo = pl.multiple_of(ff * (e % 2), ff)
+            for s in range(g2):
+                dya[g2 * e + s] = dot_tn(hid[es, s * tile:(s + 1) * tile], gy[es, :]).astype(BF16)
+            for s in range(g1):
+                xa[g1 * (e // 2) + s, :, pl.ds(lo, ff)] = dot_tn(brow[es, s * tile:(s + 1) * tile], dact[es, :]).astype(BF16)
+            for cp in weight_copies(e):
+                cp.start()
+            return carry
+        lax.fori_loop(0, 2, body, 0)
 
     for cp in pending[0]:
         cp.wait_send()
-    lax.fori_loop(0, n_cols // tok, scale_rows, 0)
+    lax.fori_loop(0, n_cols // tok // 2, scale_rows, 0)
     poll2(1, 3, 0)
+    lax.fori_loop(n_cols // tok // 2, n_cols // tok, scale_rows, 0)
+    poll2(1, 3, 1)
     chunk(0, far)
-    poll2(1, 3, 1)
     chunk(0, 3)
     ring_send2(0, 0)
     chunk(0, -3)
-    ring_send2(0, 1)
+    ring_send(0, 1, 0)
     poll2(1, 4, 0)
     poll2(1, 4, 1)
     chunk(0, 2)
+    ring_send(0, 1, 1)
     chunk(0, -2)
-    ring_send2(0, 2)
+    ring_send(0, 2, 0)
     chunk(0, 1)
+    ring_send(0, 2, 1)
+    ring_send2(0, 3)
     chunk(0, -1)
-    ring_send2(0, 3)
+    gather(1, (0, 1, -1, 2), True)
+    ring_send2(0, 4)
     chunk(0, 0)
-    gather_step(1, 0)
-    gather_step(1, -1)
-    ring_send2(0, 4)
-    for d in (1, -2, 2, -3, 3, 4):
-        gather_step(1, d)
+    gather(1, (-2, 3, -3, 4))
     ring_send2(0, 5)
     backward_pair(0)
-    ring_send2(0, 6)
     backward_pair(2)
-    emit(2, gy, gy_hbm)
-    emit(3, dact, dact_hbm)
     lax.fori_loop(0, blocks, gate_cols, 0)
     lax.fori_loop(0, n_cols // tok, flip_rows, 0)
+    ring_send2(0, 6)
     chunk(1, far)
     chunk(1, 3)
     ring_send2(1, 0)
     chunk(1, -3)
+    chunk(1, 2)
     ring_send2(1, 1)
-    chunk(1, 2)
+    finish(0, xs, xs)
+    emit(0, xs, y_hbm)
     chunk(1, -2)
     chunk(1, 1)
+    ring_send2(1, 2)
     chunk(1, -1)
-    finish(0, x_in, y_out)
-    ring_send2(1, 2)
     chunk(1, 0)
     dg_cp = send(dgt, dgs, dgb_s.at[0], dgb_r.at[0], twin)
     ring_send2(1, 3)
+    for cp in pending[1]:
+        cp.wait_send()
     landed(dgs, dgb_s.at[0], dgb_r.at[0], twin)
     dgp[...] = dgp[...] + dgs[...]
     dg_sends = [send(dgp.at[chip(d)], dgr.at[z], dg_s.at[d], dg_r.at[d], dev(chip(d), c)) for d in range(1, chips)]
+    weight_pair(0)
     ring_send2(1, 4)
+    weight_pair(2)
     ring_send2(1, 5)
-    ring_send2(1, 6)
     dg_total = dgp[z]
     for d in range(1, chips):
         landed(dgr.at[chip(-d)], dg_s.at[d], dg_r.at[d], twin)
         dg_total = dg_total + dgr[chip(-d)]
-    dg_out[...] = dg_total
-    finish(1, dy_in, dx_out)
+    dgr[z] = dg_total
+    emit(2, dgr.at[z], dg_hbm)
+    ring_send2(1, 6)
     dg_cp.wait_send()
-    for group in (dg_sends, pending[1], list(twin_wait_s.values()), *own_wait.values()):
+    for cp in dg_sends:
+        cp.wait_send()
+    for e in range(n_exp):
+        for cp in weight_copies(e):
+            cp.wait()
+    finish(1, ys, ys)
+    emit(1, ys, dx_hbm)
+    for group in (list(twin_wait_s.values()), *own_wait.values()):
         for cp in group:
             cp.wait_send()
     for cp in outs:
         cp.wait()
 
 
-def weight_kernel(y_ref, dx_ref, dg_ref, brow, hid, gy, dact, y_out, dx_out, dg_out, dw1, dw2):
-    @pl.when(pl.program_id(0) == 0)
-    def _():
-        y_out[...] = y_ref[...]
-        dx_out[...] = dx_ref[...]
-        dg_out[...] = dg_ref[...]
-
-    dw2[0] = dot_tn(hid[...], gy[...]).astype(BF16)
-    dw1[0] = dot_tn(brow[...], dact[...]).astype(BF16)
+def copy_kernel(n, *refs):
+    ins, outs, bufs, sem = refs[:n], refs[n:2 * n], refs[2 * n:3 * n], refs[3 * n]
+    jobs = []
+    for k in range(n - 1, -1, -1):
+        if ins[k].ndim == 3:
+            jobs += [(k, e, ins[k].at[e], outs[k].at[e], bufs[k].at[e]) for e in range(ins[k].shape[0])]
+        else:
+            jobs.append((k, 0, ins[k], outs[k], bufs[k]))
+    loads = [pltpu.make_async_copy(i, b, sem.at[0, k, e]) for k, e, i, o, b in jobs]
+    stores = [pltpu.make_async_copy(b, o, sem.at[1, k, e]) for k, e, i, o, b in jobs]
+    for cp in loads:
+        cp.start()
+    for ld, st in zip(loads, stores):
+        ld.wait()
+        st.start()
+    for cp in stores:
+        cp.wait()
 
 
 def solution(mesh):
@@ -537,27 +576,31 @@
         cap = (CAP_NUM * n_pairs) // (CAP_DEN * n_exp)
         rows = n_exp * cap
         chips = groups // 2
-        vmem = pl.BlockSpec(memory_space=pltpu.VMEM)
         hbm = pl.BlockSpec(memory_space=pl.ANY)
         dma = pltpu.SemaphoreType.DMA
         shape = jax.ShapeDtypeStruct
-        small = (shape((tok, dm), BF16), shape((tok, dm), BF16), shape((top_k, tok), F32))
+        outs = (shape((tok, dm), BF16), shape((tok, dm), BF16), shape((top_k, tok), F32),
+                shape((n_exp, dm, ff), BF16), shape((n_exp, ff, dm), BF16))
         mids = pl.pallas_call(
             functools.partial(moe_kernel, chips, cap, n_exp),
             name='moe',
-            out_shape=small + (shape((rows, dm), BF16), shape((rows, ff), BF16), shape((rows, dm), BF16), shape((rows, ff), BF16)),
-            in_specs=[vmem, vmem, vmem, vmem, hbm, hbm],
-            out_specs=(vmem, vmem, vmem, hbm, hbm, hbm, hbm),
+            out_shape=outs,
+            in_specs=[hbm] * 6,
+            out_specs=(hbm,) * 5,
             scratch_shapes=[
+                pltpu.VMEM((tok, dm), BF16),
+                pltpu.VMEM((tok, dm), BF16),
                 pltpu.VMEM((2, chips, top_k, tok), jnp.int32),
                 pltpu.VMEM((2, chips, top_k, tok), F32),
                 pltpu.VMEM((chips, 2 * tok, dm), BF16),
                 pltpu.VMEM((chips, 2 * tok, dm), BF16),
                 pltpu.VMEM((2 * chips, 8, tok), F32),
                 pltpu.VMEM((2 * chips, 8, tok), F32),
-                pltpu.VMEM((chips, tok, 2 * tok), BF16),
+                pltpu.VMEM((chips, 48, 2 * tok), BF16),
+                pltpu.VMEM((48, rows), F32),
+                pltpu.VMEM((8, rows), F32),
+                pltpu.VMEM((8, rows), F32),
                 pltpu.VMEM((rows, tok), F32),
-                pltpu.VMEM((rows // tok, 8, tok), F32),
                 pltpu.VMEM((rows, dm), BF16),
                 pltpu.VMEM((rows, dm), BF16),
                 pltpu.VMEM((rows, ff), BF16),
@@ -584,23 +627,18 @@
                 dma((2, 2, chips - 1)), dma((2, 2, chips - 1)),
                 dma((2, chips)), dma((2, chips)),
                 dma((chips,)), dma((chips,)), dma((1,)), dma((1,)),
-                dma((2, n_exp)), dma((4,)),
+                dma((6,)), dma((2, n_exp)), dma((3,)), dma((2, n_exp, 4)),
             ],
             compiler_params=pltpu.CompilerParams(collective_id=0, has_side_effects=True,
                                                  vmem_limit_bytes=VMEM_BYTES),
         )(expert_idx.T, gate_weight.T, x_in, grad_y, w_in, w_out)
         y, dx, dg, dw1, dw2 = pl.pallas_call(
-            weight_kernel,
-            name='weights',
-            grid=(n_exp,),
-            out_shape=small + (shape((n_exp, dm, ff), BF16), shape((n_exp, ff, dm), BF16)),
-            in_specs=[pl.BlockSpec((tok, dm), lambda e: (0, 0)), pl.BlockSpec((tok, dm), lambda e: (0, 0)),
-                      pl.BlockSpec((top_k, tok), lambda e: (0, 0)),
-                      pl.BlockSpec((cap, dm), lambda e: (e, 0)), pl.BlockSpec((cap, ff), lambda e: (e, 0)),
-                      pl.BlockSpec((cap, dm), lambda e: (e, 0)), pl.BlockSpec((cap, ff), lambda e: (e, 0))],
-            out_specs=(pl.BlockSpec((tok, dm), lambda e: (0, 0)), pl.BlockSpec((tok, dm), lambda e: (0, 0)),
-                       pl.BlockSpec((top_k, tok), lambda e: (0, 0)),
-                       pl.BlockSpec((1, dm, ff), lambda e: (e, 0, 0)), pl.BlockSpec((1, ff, dm), lambda e: (e, 0, 0))),
+            functools.partial(copy_kernel, len(outs)),
+            name='outputs',
+            out_shape=outs,
+            in_specs=[hbm] * len(outs),
+            out_specs=(hbm,) * len(outs),
+            scratch_shapes=[pltpu.VMEM(o.shape, o.dtype) for o in outs] + [dma((2, len(outs), n_exp))],
         )(*mids)
         return y, dx, dg.T, dw1, dw2
 

time: 157 us -> 151 us (0.962)
  Pallas kernels: 156 us -> 150 us
    pallas_call x1, Pallas kernels: 147 us -> 143 us  [device_pass(): pl.pallas_call(functools.partial(moe_kernel, chips, cap, n_exp), name='mo...]
    pallas_call x1, Pallas kernels: 8.96 us -> 6.81 us  [device_pass(): pl.pallas_call(functools.partial(copy_kernel, len(outs)), name='outputs',...]
where the time goes in v1:
time: 151 us
  Pallas kernels  150 us (99%)
    pallas_call x1, Pallas kernels, device_pass(): pl.pallas_call(functools.partial(moe_kernel, chips, cap, n_exp), name='mo...  143 us
    pallas_call x1, Pallas kernels, device_pass(): pl.pallas_call(functools.partial(copy_kernel, len(outs)), name='outputs',...  6.81 us

profile of v1, /device:TPU:21, one launch (start us, length us, event | category | flops | bytes accessed | tf_op | source)
XLA Modules:
  0.0 150.9 jit_solution(13769859631774533056)
XLA Ops:
  0.6 143.3 %moe.1 = (bf16[128,1024]{1,0:T(8,128)(2,1)}, bf16[128,1024]{1,0:T(8,128)(2,1)}, f32[8,128]{1,0:T(8,128)}, bf16[4,1024,512]{2,1,0:T(8,128)(2,1)}, bf16[4,512,1024]{2,1,0:T(8,128)(2,1)}) custom-call(s32[8,128]{1,0:T(8,128)} %bitcast.3, f32[8,128]{1,0:T(8,128)} %bitcast.4, bf16[128,1024]{1,0:T(8,128)(2,1)} %x_hbm.1, bf16[128,1024]{1,0:T(8,128)(2,1)} %dy_hbm.1, ...), custom_call_target="tpu_custom_call" | custom-call | tf_op jit(solution)/shard_map/moe/pallas_call | solution.py:584
  143.9 6.8 %outputs.1 = (bf16[128,1024]{1,0:T(8,128)(2,1)}, bf16[128,1024]{1,0:T(8,128)(2,1)}, f32[8,128]{1,0:T(8,128)}, bf16[4,1024,512]{2,1,0:T(8,128)(2,1)}, bf16[4,512,1024]{2,1,0:T(8,128)(2,1)}) custom-call(bf16[128,1024]{1,0:T(8,128)(2,1)} %get-tuple-element.15.refs_0_, bf16[128,1024]{1,0:T(8,128)(2,1)} %get-tuple-element.16.refs_1_, ...), custom_call_target="tpu_custom_call" | custom-call | tf_op jit(solution)/shard_map/outputs/pallas_call | solution.py:635

commit v2 on v1

--- a/solution.py
+++ b/solution.py
@@ -47,8 +47,8 @@
 def moe_kernel(chips, cap, n_exp,
                idx_hbm, gate_hbm, x_hbm, dy_hbm, w1_hbm, w2_hbm,
                y_hbm, dx_hbm, dg_hbm, dw1_hbm, dw2_hbm,
-               xs, ys, idx_all, gate_all, xa, dya, vt, cnt, tab, ft, hitm, grow, gcol, brow, gy, hid, slope, orow, dact,
-               pick, go, tail, part, spare, sib, ring, mgt, dgp, dgt, dgs, dgr, w1, w2,
+               xs, ys, idx_all, gate_all, xa, dya, vt, cnt, tab, ft, hitm, grow, gcol, gpart, brow, gy, hid, slope, orow, dact,
+               pick, go, part, spare, sib, ring, mgt, dgp, dgt, dgs, dgr, w1, w2,
                ag_s, ag_r, agb_s, agb_r, in_s, in_r, inb_s, inb_r, rs_s, rs_r, rsb_s, rsb_r,
                dg_s, dg_r, dgb_s, dgb_r, l_sem, w_sem, o_sem, dw_sem):
     top_k, tok = idx_all.shape[2:]
@@ -96,7 +96,7 @@
         inputs.append(cp)
 
     barrier = pltpu.get_barrier_semaphore()
-    for d in range(1, chips):
+    for d in sorted(range(1, chips), key=lambda d: -min(d, chips - d)):
         pl.semaphore_signal(barrier, inc=1, device_id=dev(chip(d), c), device_id_type=MESH)
     pl.semaphore_signal(barrier, inc=1, device_id=twin, device_id_type=MESH)
 
@@ -250,7 +250,10 @@
 
     def gate_col(i, carry):
         sl = pl.ds(pl.multiple_of(i * tok, tok), tok)
-        gcol[sl, :] = jnp.transpose(jnp.broadcast_to(grow[0:1, sl], (tok, tok)))
+        v = jnp.transpose(jnp.broadcast_to(grow[0:1, sl], (tok, tok)))
+        gcol[sl, :] = v
+        for s, w in enumerate(split3(v)):
+            gpart[s, sl, :] = w.astype(BF16)
         return carry
 
     lax.fori_loop(0, rows // tok, gate_col, 0)
@@ -310,27 +313,11 @@
     own_wait, twin_wait_s = {}, {}
     n_cols = xs.shape[1]
     tile = xa.shape[1]
-    wide = xa.shape[2]
+    step = 2 * tile
     blocks = rows // tok
-    main = wide // tok
 
     def mtile(m):
-        return pl.ds(pl.multiple_of(m * tile, tile), tile)
-
-    def scale_rows(j, carry):
-        js = pl.ds(pl.multiple_of(j * tok, tok), tok)
-        m = j // (tile // tok)
-        ms = pl.ds(pl.multiple_of((j % (tile // tok)) * tok, tok), tok)
-        for i in range(blocks):
-            t = jnp.transpose(orow[i * tok:(i + 1) * tok, js]).astype(F32)
-            hi, mid, lo = split3(t * grow[0:1, i * tok:(i + 1) * tok])
-            go[js, i * tok:(i + 1) * tok] = hi.astype(BF16)
-            for s, v in enumerate((mid, lo)):
-                if i < main:
-                    xa[s * (n_cols // tile) + m, ms, i * tok:(i + 1) * tok] = v.astype(BF16)
-                else:
-                    tail[s, js, (i - main) * tok:(i - main + 1) * tok] = v.astype(BF16)
-        return carry
+        return pl.ds(pl.multiple_of(m * step, step), step)
 
     def flip_rows(j, carry):
         js = pl.ds(pl.multiple_of(j * tok, tok), tok)
@@ -346,19 +333,33 @@
         if sp in twin_wait_s:
             twin_wait_s.pop(sp).wait_send()
 
+        per = tile // tok
+        if a == 0:
+            def scale(i, carry):
+                sl = pl.ds(pl.multiple_of(i * tok, tok), tok)
+                sub = pl.ds(pl.multiple_of((i % per) * tok, tok), tok)
+                for s in range(3):
+                    g = gpart[s, sl, :]
+                    xa[i // per, sub, s * 2 * tok:(s + 1) * 2 * tok] = pick[q, sl, :] * jnp.concatenate([g, g], axis=1)
+                return carry
+            lax.fori_loop(0, blocks, scale, 0)
+
         def body(m, carry):
             ms = mtile(m)
-            r = dot_nn(go[ms, :], pick[q])
             if a == 0:
-                for s in range(2):
-                    r = r + dot_nn(xa[s * (n_cols // tile) + m], pick[q, 0:wide, :])
-                    r = r + dot_nn(tail[s, ms, :], pick[q, wide:rows, :])
+                r = None
+                for s in range(3):
+                    w = xa[0:rows // tile, :, s * 2 * tok:(s + 1) * 2 * tok].reshape(rows, 2 * tok)
+                    t = dot_nn(go[ms, :], w)
+                    r = t if r is None else r + t
+            else:
+                r = dot_nn(go[ms, :], pick[q])
             r0, r1 = r[:, 0:tok], r[:, tok:2 * tok]
             part[di, ms, :] = jnp.where(c == 0, r0, r1)
             spare[sp, ms, :] = jnp.where(c == 0, r1, r0)
             return carry
 
-        lax.fori_loop(0, n_cols // tile, body, 0)
+        lax.fori_loop(0, n_cols // step, body, 0)
         twin_wait_s[sp] = send(spare.at[sp], sib.at[a, di], rsb_s.at[a, di], rsb_r.at[a, di], twin)
         if a == 1:
             t = dot_nn(mgt[...], pick[q])
@@ -467,13 +468,12 @@
             return carry
         lax.fori_loop(0, 2, body, 0)
 
+    lax.fori_loop(0, n_cols // tok, flip_rows, 0)
+    poll2(1, 3, 0)
     for cp in pending[0]:
         cp.wait_send()
-    lax.fori_loop(0, n_cols // tok // 2, scale_rows, 0)
-    poll2(1, 3, 0)
-    lax.fori_loop(n_cols // tok // 2, n_cols // tok, scale_rows, 0)
+    chunk(0, far)
     poll2(1, 3, 1)
-    chunk(0, far)
     chunk(0, 3)
     ring_send2(0, 0)
     chunk(0, -3)
@@ -601,6 +601,7 @@
                 pltpu.VMEM((8, rows), F32),
                 pltpu.VMEM((8, rows), F32),
                 pltpu.VMEM((rows, tok), F32),
+                pltpu.VMEM((3, rows, tok), BF16),
                 pltpu.VMEM((rows, dm), BF16),
                 pltpu.VMEM((rows, dm), BF16),
                 pltpu.VMEM((rows, ff), BF16),
@@ -609,7 +610,6 @@
                 pltpu.VMEM((rows, ff), BF16),
                 pltpu.VMEM((chips, rows, 2 * tok), BF16),
                 pltpu.VMEM((dm, rows), BF16),
-                pltpu.VMEM((2, dm, rows - dm), BF16),
                 pltpu.VMEM((chips, dm, tok), F32),
                 pltpu.VMEM((4, dm, tok), F32),
                 pltpu.VMEM((2, chips, dm, tok), F32),

time: 151 us -> 149 us (0.987)
  Pallas kernels: 150 us -> 148 us
    pallas_call x1, Pallas kernels: 143 us -> 141 us  [device_pass(): pl.pallas_call(functools.partial(moe_kernel, chips, cap, n_exp), name='mo...]
where the time goes in v2:
time: 149 us
  Pallas kernels  148 us (99%)
    pallas_call x1, Pallas kernels, device_pass(): pl.pallas_call(functools.partial(moe_kernel, chips, cap, n_exp), name='mo...  141 us
    pallas_call x1, Pallas kernels, device_pass(): pl.pallas_call(functools.partial(copy_kernel, len(outs)), name='outputs',...  6.81 us

profile of v2, /device:TPU:21, one launch (start us, length us, event | category | flops | bytes accessed | tf_op | source)
XLA Modules:
  0.0 148.7 jit_solution(17492349899345895173)
XLA Ops:
  0.6 141.1 %moe.1 = (bf16[128,1024]{1,0:T(8,128)(2,1)}, bf16[128,1024]{1,0:T(8,128)(2,1)}, f32[8,128]{1,0:T(8,128)}, bf16[4,1024,512]{2,1,0:T(8,128)(2,1)}, bf16[4,512,1024]{2,1,0:T(8,128)(2,1)}) custom-call(s32[8,128]{1,0:T(8,128)} %bitcast.3, f32[8,128]{1,0:T(8,128)} %bitcast.4, bf16[128,1024]{1,0:T(8,128)(2,1)} %x_hbm.1, bf16[128,1024]{1,0:T(8,128)(2,1)} %dy_hbm.1, ...), custom_call_target="tpu_custom_call" | custom-call | tf_op jit(solution)/shard_map/moe/pallas_call | solution.py:584
  141.7 6.8 %outputs.1 = (bf16[128,1024]{1,0:T(8,128)(2,1)}, bf16[128,1024]{1,0:T(8,128)(2,1)}, f32[8,128]{1,0:T(8,128)}, bf16[4,1024,512]{2,1,0:T(8,128)(2,1)}, bf16[4,512,1024]{2,1,0:T(8,128)(2,1)}) custom-call(bf16[128,1024]{1,0:T(8,128)(2,1)} %get-tuple-element.15.refs_0_, bf16[128,1024]{1,0:T(8,128)(2,1)} %get-tuple-element.16.refs_1_, ...), custom_call_target="tpu_custom_call" | custom-call | tf_op jit(solution)/shard_map/outputs/pallas_call | solution.py:635

commit v3 on v2

--- a/solution.py
+++ b/solution.py
@@ -15,7 +15,7 @@
 K0 = 0.7978845608028654
 K1 = 0.044715
 MESH = pl.DeviceIdType.MESH
-VMEM_BYTES = 67_000_000
+VMEM_BYTES = 57_900_000
 
 
 def split3(v):
@@ -46,11 +46,11 @@
 
 def moe_kernel(chips, cap, n_exp,
                idx_hbm, gate_hbm, x_hbm, dy_hbm, w1_hbm, w2_hbm,
-               y_hbm, dx_hbm, dg_hbm, dw1_hbm, dw2_hbm,
-               xs, ys, idx_all, gate_all, xa, dya, vt, cnt, tab, ft, hitm, grow, gcol, gpart, brow, gy, hid, slope, orow, dact,
-               pick, go, part, spare, sib, ring, mgt, dgp, dgt, dgs, dgr, w1, w2,
+               xs, ys, dgs, xa, dya,
+               idx_all, gate_all, vt, cnt, tab, ft, hitm, grow, gcol, gpart, brow, gy, hid, slope, orow, dact,
+               pick, go, part, spare, sib, ring, mgt, dgp, dgt, dgr, w1, w2,
                ag_s, ag_r, agb_s, agb_r, in_s, in_r, inb_s, inb_r, rs_s, rs_r, rsb_s, rsb_r,
-               dg_s, dg_r, dgb_s, dgb_r, l_sem, w_sem, o_sem, dw_sem):
+               dg_s, dg_r, dgb_s, dgb_r, l_sem, w_sem):
     top_k, tok = idx_all.shape[2:]
     half = tok // 2
     rows = n_exp * cap
@@ -68,13 +68,6 @@
     right, left, twin = dev(chip(1), c), dev(chip(-1), c), {'expert': z * 2 + 1 - c}
     side = (right, left)
     pending = ([], [])
-    outs = []
-
-    def emit(k, src, dst):
-        cp = pltpu.make_async_copy(src, dst, o_sem.at[k])
-        cp.start()
-        outs.append(cp)
-
     def rcopy(src, dst, ss, rs, to):
         return pltpu.make_async_remote_copy(src_ref=src, dst_ref=dst, send_sem=ss, recv_sem=rs,
                                             device_id=to, device_id_type=MESH)
@@ -444,16 +437,6 @@
     ff = w1.shape[2]
     g1, g2 = n_cols // tile, ff // tile
 
-    def weight_copies(e):
-        lo = pl.multiple_of(ff * (e % 2), ff)
-        out = []
-        for s in range(g2):
-            out.append(pltpu.make_async_copy(dya.at[g2 * e + s], dw2_hbm.at[e, pl.ds(s * tile, tile)], dw_sem.at[0, e, s]))
-        for s in range(g1):
-            out.append(pltpu.make_async_copy(xa.at[g1 * (e // 2) + s, :, pl.ds(lo, ff)],
-                                             dw1_hbm.at[e, pl.ds(s * tile, tile)], dw_sem.at[1, e, s]))
-        return out
-
     def weight_pair(e0):
         def body(i, carry):
             e = e0 + i
@@ -463,8 +446,6 @@
                 dya[g2 * e + s] = dot_tn(hid[es, s * tile:(s + 1) * tile], gy[es, :]).astype(BF16)
             for s in range(g1):
                 xa[g1 * (e // 2) + s, :, pl.ds(lo, ff)] = dot_tn(brow[es, s * tile:(s + 1) * tile], dact[es, :]).astype(BF16)
-            for cp in weight_copies(e):
-                cp.start()
             return carry
         lax.fori_loop(0, 2, body, 0)
 
@@ -505,7 +486,6 @@
     chunk(1, 2)
     ring_send2(1, 1)
     finish(0, xs, xs)
-    emit(0, xs, y_hbm)
     chunk(1, -2)
     chunk(1, 1)
     ring_send2(1, 2)
@@ -526,40 +506,30 @@
     for d in range(1, chips):
         landed(dgr.at[chip(-d)], dg_s.at[d], dg_r.at[d], twin)
         dg_total = dg_total + dgr[chip(-d)]
-    dgr[z] = dg_total
-    emit(2, dgr.at[z], dg_hbm)
+    dgs[0] = dg_total
     ring_send2(1, 6)
     dg_cp.wait_send()
     for cp in dg_sends:
         cp.wait_send()
-    for e in range(n_exp):
-        for cp in weight_copies(e):
-            cp.wait()
     finish(1, ys, ys)
-    emit(1, ys, dx_hbm)
     for group in (list(twin_wait_s.values()), *own_wait.values()):
         for cp in group:
             cp.wait_send()
-    for cp in outs:
-        cp.wait()
-
-
-def copy_kernel(n, *refs):
-    ins, outs, bufs, sem = refs[:n], refs[n:2 * n], refs[2 * n:3 * n], refs[3 * n]
-    jobs = []
-    for k in range(n - 1, -1, -1):
-        if ins[k].ndim == 3:
-            jobs += [(k, e, ins[k].at[e], outs[k].at[e], bufs[k].at[e]) for e in range(ins[k].shape[0])]
-        else:
-            jobs.append((k, 0, ins[k], outs[k], bufs[k]))
-    loads = [pltpu.make_async_copy(i, b, sem.at[0, k, e]) for k, e, i, o, b in jobs]
-    stores = [pltpu.make_async_copy(b, o, sem.at[1, k, e]) for k, e, i, o, b in jobs]
-    for cp in loads:
+
+
+def copy_kernel(xs, ys, dgs, xa, dya, y, dx, dg, dw1, dw2, sem):
+    n_exp, n_cols, ff = dw1.shape
+    tile = xa.shape[1]
+    g1, g2 = n_cols // tile, ff // tile
+    jobs = [(xs, y), (ys, dx), (dgs.at[0], dg)]
+    for e in range(n_exp):
+        lo = ff * (e % 2)
+        jobs += [(dya.at[g2 * e + s], dw2.at[e, pl.ds(s * tile, tile)]) for s in range(g2)]
+        jobs += [(xa.at[g1 * (e // 2) + s, :, pl.ds(lo, ff)], dw1.at[e, pl.ds(s * tile, tile)]) for s in range(g1)]
+    copies = [pltpu.make_async_copy(a, b, sem.at[k]) for k, (a, b) in enumerate(jobs)]
+    for cp in copies:
         cp.start()
-    for ld, st in zip(loads, stores):
-        ld.wait()
-        st.start()
-    for cp in stores:
+    for cp in copies:
         cp.wait()
 
 
@@ -581,19 +551,18 @@
         shape = jax.ShapeDtypeStruct
         outs = (shape((tok, dm), BF16), shape((tok, dm), BF16), shape((top_k, tok), F32),
                 shape((n_exp, dm, ff), BF16), shape((n_exp, ff, dm), BF16))
-        mids = pl.pallas_call(
+        vmem = pl.BlockSpec(memory_space=pltpu.VMEM)
+        mids = (pltpu.VMEM((tok, dm), BF16), pltpu.VMEM((tok, dm), BF16), pltpu.VMEM((chips, top_k, tok), F32),
+                pltpu.VMEM((chips, 2 * tok, dm), BF16), pltpu.VMEM((chips, 2 * tok, dm), BF16))
+        held = pl.pallas_call(
             functools.partial(moe_kernel, chips, cap, n_exp),
             name='moe',
-            out_shape=outs,
+            out_shape=mids,
             in_specs=[hbm] * 6,
-            out_specs=(hbm,) * 5,
+            out_specs=(vmem,) * 5,
             scratch_shapes=[
-                pltpu.VMEM((tok, dm), BF16),
-                pltpu.VMEM((tok, dm), BF16),
                 pltpu.VMEM((2, chips, top_k, tok), jnp.int32),
                 pltpu.VMEM((2, chips, top_k, tok), F32),
-                pltpu.VMEM((chips, 2 * tok, dm), BF16),
-                pltpu.VMEM((chips, 2 * tok, dm), BF16),
                 pltpu.VMEM((2 * chips, 8, tok), F32),
                 pltpu.VMEM((2 * chips, 8, tok), F32),
                 pltpu.VMEM((chips, 48, 2 * tok), BF16),
@@ -618,7 +587,6 @@
                 pltpu.VMEM((chips, 8, tok), F32),
                 pltpu.VMEM((chips, 8, tok), F32),
                 pltpu.VMEM((chips, 8, tok), F32),
-                pltpu.VMEM((chips, 8, tok), F32),
                 pltpu.VMEM((n_exp, dm, ff), BF16),
                 pltpu.VMEM((n_exp, ff, dm), BF16),
                 dma((2, 2, chips - 1)), dma((2, 2, chips - 1)),
@@ -627,19 +595,20 @@
                 dma((2, 2, chips - 1)), dma((2, 2, chips - 1)),
                 dma((2, chips)), dma((2, chips)),
                 dma((chips,)), dma((chips,)), dma((1,)), dma((1,)),
-                dma((6,)), dma((2, n_exp)), dma((3,)), dma((2, n_exp, 4)),
+                dma((6,)), dma((2, n_exp)),
             ],
             compiler_params=pltpu.CompilerParams(collective_id=0, has_side_effects=True,
                                                  vmem_limit_bytes=VMEM_BYTES),
         )(expert_idx.T, gate_weight.T, x_in, grad_y, w_in, w_out)
         y, dx, dg, dw1, dw2 = pl.pallas_call(
-            functools.partial(copy_kernel, len(outs)),
+            copy_kernel,
             name='outputs',
             out_shape=outs,
-            in_specs=[hbm] * len(outs),
+            in_specs=[vmem] * len(mids),
             out_specs=(hbm,) * len(outs),
-            scratch_shapes=[pltpu.VMEM(o.shape, o.dtype) for o in outs] + [dma((2, len(outs), n_exp))],
-        )(*mids)
+            scratch_shapes=[dma((3 + n_exp * (dm + ff) // (2 * tok),))],
+            compiler_params=pltpu.CompilerParams(vmem_limit_bytes=1 << 20),
+        )(*[pltpu.with_memory_space_constraint(v, pltpu.VMEM) for v in held])
         return y, dx, dg.T, dw1, dw2
 
     return jax.shard_map(device_pass, mesh=mesh,

time: 149 us -> 145 us (0.973)
  Pallas kernels: 148 us -> 144 us
    pallas_call x1, Pallas kernels: 6.81 us -> 3.66 us  [device_pass(): pl.pallas_call(copy_kernel, name='outputs', out_shape=outs, in_specs=[vme...]
where the time goes in v3:
time: 145 us
  Pallas kernels  144 us (99%)
    pallas_call x1, Pallas kernels, device_pass(): pl.pallas_call(functools.partial(moe_kernel, chips, cap, n_exp), name='mo...  140 us
    pallas_call x1, Pallas kernels, device_pass(): pl.pallas_call(copy_kernel, name='outputs', out_shape=outs, in_specs=[vme...  3.66 us

profile of v3, /device:TPU:21, one launch (start us, length us, event | category | flops | bytes accessed | tf_op | source)
XLA Modules:
  0.0 144.6 jit_solution(11882540557017838876)
XLA Ops:
  0.6 140.1 %moe.1 = (bf16[128,1024]{1,0:T(8,128)(2,1)S(1)}, bf16[128,1024]{1,0:T(8,128)(2,1)S(1)}, f32[8,8,128]{2,1,0:T(8,128)S(1)}, bf16[8,256,1024]{2,1,0:T(8,128)(2,1)S(1)}, bf16[8,256,1024]{2,1,0:T(8,128)(2,1)S(1)}) custom-call(s32[8,128]{1,0:T(8,128)} %bitcast.3, f32[8,128]{1,0:T(8,128)} %bitcast.4, bf16[128,1024]{1,0:T(8,128)(2,1)} %x_hbm.1, ...), custom_call_target="tpu_custom_call" | custom-call | tf_op jit(solution)/shard_map/moe/pallas_call | solution.py:557
  140.8 3.7 %outputs.1 = (bf16[128,1024]{1,0:T(8,128)(2,1)}, bf16[128,1024]{1,0:T(8,128)(2,1)}, f32[8,128]{1,0:T(8,128)}, bf16[4,1024,512]{2,1,0:T(8,128)(2,1)}, bf16[4,512,1024]{2,1,0:T(8,128)(2,1)}) custom-call(bf16[128,1024]{1,0:T(8,128)(2,1)S(1)} %get-tuple-element.15.xs, bf16[128,1024]{1,0:T(8,128)(2,1)S(1)} %get-tuple-element.16.ys, ...), custom_call_target="tpu_custom_call" | custom-call | tf_op jit(solution)/shard_map/outputs/pallas_call | solution.py:603

commit v4 on v3

--- a/solution.py
+++ b/solution.py
@@ -273,10 +273,12 @@
     gather(0, (2, -2))
     poll2(0, 3, 1)
     poll2(1, 1, 0)
+    gather(0, (3, -3))
     poll2(0, 4, 0)
     poll2(0, 4, 1)
     poll2(1, 1, 1)
-    gather(0, (3, -3, 4))
+    poll2(1, 2, 0)
+    gather(0, (4,))
 
     for cp in loads:
         cp.wait()
@@ -293,9 +295,8 @@
         lax.fori_loop(0, 2, body, 0)
 
     forward_pair(0)
-    poll2(1, 2, 0)
+    poll2(1, 2, 1)
     forward_pair(2)
-    poll2(1, 2, 1)
 
     order = [far]
     for d in range(far - 1, 0, -1):

time: 145 us -> 142 us (0.979)
  Pallas kernels: 144 us -> 141 us
    pallas_call x1, Pallas kernels: 140 us -> 137 us  [device_pass(): pl.pallas_call(functools.partial(moe_kernel, chips, cap, n_exp), name='mo...]
where the time goes in v4:
time: 142 us
  Pallas kernels  141 us (99%)
    pallas_call x1, Pallas kernels, device_pass(): pl.pallas_call(functools.partial(moe_kernel, chips, cap, n_exp), name='mo...  137 us
    pallas_call x1, Pallas kernels, device_pass(): pl.pallas_call(copy_kernel, name='outputs', out_shape=outs, in_specs=[vme...  3.66 us

profile of v4, /device:TPU:21, one launch (start us, length us, event | category | flops | bytes accessed | tf_op | source)
XLA Modules:
  0.0 141.7 jit_solution(14178072716951183231)
XLA Ops:
  0.6 137.3 %moe.1 = (bf16[128,1024]{1,0:T(8,128)(2,1)S(1)}, bf16[128,1024]{1,0:T(8,128)(2,1)S(1)}, f32[8,8,128]{2,1,0:T(8,128)S(1)}, bf16[8,256,1024]{2,1,0:T(8,128)(2,1)S(1)}, bf16[8,256,1024]{2,1,0:T(8,128)(2,1)S(1)}) custom-call(s32[8,128]{1,0:T(8,128)} %bitcast.3, f32[8,128]{1,0:T(8,128)} %bitcast.4, bf16[128,1024]{1,0:T(8,128)(2,1)} %x_hbm.1, ...), custom_call_target="tpu_custom_call" | custom-call | tf_op jit(solution)/shard_map/moe/pallas_call | solution.py:558
  137.9 3.7 %outputs.1 = (bf16[128,1024]{1,0:T(8,128)(2,1)}, bf16[128,1024]{1,0:T(8,128)(2,1)}, f32[8,128]{1,0:T(8,128)}, bf16[4,1024,512]{2,1,0:T(8,128)(2,1)}, bf16[4,512,1024]{2,1,0:T(8,128)(2,1)}) custom-call(bf16[128,1024]{1,0:T(8,128)(2,1)S(1)} %get-tuple-element.15.xs, bf16[128,1024]{1,0:T(8,128)(2,1)S(1)} %get-tuple-element.16.ys, ...), custom_call_target="tpu_custom_call" | custom-call | tf_op jit(solution)/shard_map/outputs/pallas_call | solution.py:604

commit v5 on v4

--- a/solution.py
+++ b/solution.py
@@ -123,8 +123,8 @@
             landed(slot(a, chip(d), h, 1 - c), agb_s.at[a, di, h], agb_r.at[a, di, h], twin)
 
     def first_send(a, h):
-        src = own[a].at[pl.ds(h * half, half)]
-        for r in range(2):
+        for r, h in enumerate((h, 1 - h)):
+            src = own[a].at[pl.ds(h * half, half)]
             i = item(1, h)
             pending[a].append(send(src, slot(a, z, h), ag_s.at[a, r, i], ag_r.at[a, r, i], side[r]))
 
@@ -143,7 +143,7 @@
             poll(a, k, h, h)
         else:
             poll(a, k, h, 0)
-            poll(a, k, h, 1)
+            poll(a, k, 1 - h, 1)
 
     small = (idx_all, gate_all)
     for d in range(1, chips):
@@ -319,13 +319,18 @@
             go[js, i * tok:(i + 1) * tok] = jnp.transpose(orow[i * tok:(i + 1) * tok, js])
         return carry
 
+    def twin_copy(a, di, sp, m):
+        ms = mtile(m)
+        return rcopy(spare.at[sp, ms], sib.at[a, di, ms], rsb_s.at[a, di, m], rsb_r.at[a, di, m], twin)
+
     def chunk(a, d):
         q, di = chip(d), place[d]
         sp = di % spare.shape[0]
         for cp in own_wait.pop(di, []):
             cp.wait_send()
         if sp in twin_wait_s:
-            twin_wait_s.pop(sp).wait_send()
+            for cp in twin_wait_s.pop(sp):
+                cp.wait_send()
 
         per = tile // tok
         if a == 0:
@@ -351,10 +356,11 @@
             r0, r1 = r[:, 0:tok], r[:, tok:2 * tok]
             part[di, ms, :] = jnp.where(c == 0, r0, r1)
             spare[sp, ms, :] = jnp.where(c == 0, r1, r0)
+            twin_copy(a, di, sp, m).start()
             return carry
 
         lax.fori_loop(0, n_cols // step, body, 0)
-        twin_wait_s[sp] = send(spare.at[sp], sib.at[a, di], rsb_s.at[a, di], rsb_r.at[a, di], twin)
+        twin_wait_s[sp] = [twin_copy(a, di, sp, m) for m in range(n_cols // step)]
         if a == 1:
             t = dot_nn(mgt[...], pick[q])
             t = t[0:8] + t[8:16] + t[16:24]
@@ -368,11 +374,11 @@
 
     seen = set()
 
-    def twin_part_wait(a, d):
+    def twin_part_wait(a, d, h):
         di = place[d]
-        if (a, di) not in seen:
-            seen.add((a, di))
-            landed(sib.at[a, di], rsb_s.at[a, di], rsb_r.at[a, di], twin)
+        if (a, di, h) not in seen:
+            seen.add((a, di, h))
+            landed(sib.at[a, di, pl.ds(h * hd, hd)], rsb_s.at[a, di, h], rsb_r.at[a, di, h], twin)
 
     def items(r):
         near, other = (0, 1) if r == 0 else (1, 0)
@@ -385,7 +391,7 @@
         d, h = items(r)[i]
         sd = d if r == 0 else -d
         di = place[sd]
-        twin_part_wait(a, sd)
+        twin_part_wait(a, sd, h)
         ref = mine(sd, h)
         total = ref[...] + sib[a, di, h * hd:(h + 1) * hd, :]
         if (d + 1, h) in items(r):
@@ -400,8 +406,8 @@
         ring_send(a, i, 1)
 
     def finish(a, src, dst):
-        twin_part_wait(a, 0)
         for h in range(2):
+            twin_part_wait(a, 0, h)
             total = mine(0, h)[...] + sib[a, place[0], h * hd:(h + 1) * hd, :]
             for r in range(2):
                 p = items(r).index((1, h))
@@ -513,7 +519,7 @@
     for cp in dg_sends:
         cp.wait_send()
     finish(1, ys, ys)
-    for group in (list(twin_wait_s.values()), *own_wait.values()):
+    for group in (*twin_wait_s.values(), *own_wait.values()):
         for cp in group:
             cp.wait_send()
 
@@ -594,7 +600,7 @@
                 dma((2, chips, 2)), dma((2, chips, 2)),
                 dma((2, chips)), dma((2, chips)), dma((2,)), dma((2,)),
                 dma((2, 2, chips - 1)), dma((2, 2, chips - 1)),
-                dma((2, chips)), dma((2, chips)),
+                dma((2, chips, 2)), dma((2, chips, 2)),
                 dma((chips,)), dma((chips,)), dma((1,)), dma((1,)),
                 dma((6,)), dma((2, n_exp)),
             ],

time: 142 us -> 142 us (level)
  no operation moved by 1% of the time
where the time goes in v5:
time: 142 us; the launch traced here: 140 us
  Pallas kernels  140 us (99%)
    pallas_call x1, Pallas kernels, device_pass(): pl.pallas_call(functools.partial(moe_kernel, chips, cap, n_exp), name='mo...  136 us
    pallas_call x1, Pallas kernels, device_pass(): pl.pallas_call(copy_kernel, name='outputs', out_shape=outs, in_specs=[vme...  3.66 us

profile of v5, /device:TPU:21, one launch (start us, length us, event | category | flops | bytes accessed | tf_op | source)
XLA Modules:
  0.0 140.4 jit_solution(4255439143709989538)
XLA Ops:
  0.6 136.0 %moe.1 = (bf16[128,1024]{1,0:T(8,128)(2,1)S(1)}, bf16[128,1024]{1,0:T(8,128)(2,1)S(1)}, f32[8,8,128]{2,1,0:T(8,128)S(1)}, bf16[8,256,1024]{2,1,0:T(8,128)(2,1)S(1)}, bf16[8,256,1024]{2,1,0:T(8,128)(2,1)S(1)}) custom-call(s32[8,128]{1,0:T(8,128)} %bitcast.3, f32[8,128]{1,0:T(8,128)} %bitcast.4, bf16[128,1024]{1,0:T(8,128)(2,1)} %x_hbm.1, ...), custom_call_target="tpu_custom_call" | custom-call | tf_op jit(solution)/shard_map/moe/pallas_call | solution.py:564
  136.6 3.7 %outputs.1 = (bf16[128,1024]{1,0:T(8,128)(2,1)}, bf16[128,1024]{1,0:T(8,128)(2,1)}, f32[8,128]{1,0:T(8,128)}, bf16[4,1024,512]{2,1,0:T(8,128)(2,1)}, bf16[4,512,1024]{2,1,0:T(8,128)(2,1)}) custom-call(bf16[128,1024]{1,0:T(8,128)(2,1)S(1)} %get-tuple-element.15.xs, bf16[128,1024]{1,0:T(8,128)(2,1)S(1)} %get-tuple-element.16.ys, ...), custom_call_target="tpu_custom_call" | custom-call | tf_op jit(solution)/shard_map/outputs/pallas_call | solution.py:610
